TPU v7x, 32 devices: a whole 2x2x4 slice. The times are simulated.
32 devices in a mesh: dp: 4 (over y, x), expert: 8 (over z, core).
Axes of the slice: x: 2, y: 2, z: 4, core: 2. Of those that a mesh axis runs over, the one named last changes fastest.
Arguments:
- tokens: bfloat16 [4096, 2048], P(('dp', 'expert')), may hold values from -6 to 6
- routes: int32 [4096, 8], P(('dp', 'expert')), may hold values from 0 to 15, all different within a row
- route_weight: float32 [4096, 8], P(('dp', 'expert')), may hold values from 0.05 to 0.5
- bias: float32 [16], replicated, may hold values from -3 to 3
- w_gate: bfloat16 [16, 768, 2048], P('expert', 'dp'), may hold values from -0.125 to 0.125
- w_up: bfloat16 [16, 768, 2048], P('expert', 'dp'), may hold values from -0.125 to 0.125
- w_down: bfloat16 [16, 768, 2048], P('expert', 'dp'), may hold values from -0.21875 to 0.21875
Outputs:
- mixed: bfloat16 [4096, 2048], P(('dp', 'expert'))
- new_bias: float32 [16], replicated
- counts: int32 [16], replicated
Inputs may be any that keep to these rules, and one draw needn't show every extreme that they name: `routes`: each token names 8 different experts.
All inputs are finite; a program needn't handle non-finite values.
Results may differ from a plain program's by a relative error of at most 0.0057.
Values may be sent and summed in bfloat16 or wider, within the bound.
A program may use at most 128 MiB of HBM per device.

v0:
```python
import jax
import jax.numpy as jnp
from jax import lax
from jax.sharding import PartitionSpec as P

bias_rate = 0.05


def expert_products(received, gate_w, up_w, down_w):
    gate_act = jnp.einsum("sjcd,jfd->sjcf", received, gate_w, preferred_element_type=jnp.float32)
    up_act = jnp.einsum("sjcd,jfd->sjcf", received, up_w, preferred_element_type=jnp.float32)
    hidden = (jax.nn.silu(gate_act) * up_act).astype(jnp.bfloat16)
    return jnp.einsum("sjcf,jfd->sjcd", hidden, down_w, preferred_element_type=jnp.float32)


def body(tokens, routes, route_weight, bias, w_gate, w_up, w_down):
    tok_rows, feature_width = tokens.shape
    top_count = routes.shape[1]
    experts = bias.shape[0]
    groups = lax.axis_size("expert")
    per_device = w_gate.shape[0]
    capacity = 5 * tok_rows * top_count // (4 * experts)
    flat_routes = routes.reshape(-1)
    labels = jnp.arange(experts, dtype=jnp.int32)
    picked = (flat_routes[:, None] == labels[None, :]).astype(jnp.int32)
    running = jnp.cumsum(picked, axis=0) - picked
    slot_rank = jnp.sum(running * picked, axis=1)
    local_counts = jnp.sum(picked, axis=0)
    kept_mask = slot_rank < capacity
    slot_total = experts * capacity
    slot_index = jnp.where(kept_mask, flat_routes * capacity + slot_rank, slot_total)
    token_index = jnp.arange(tok_rows * top_count, dtype=jnp.int32) // top_count
    source = jnp.zeros((slot_total + 1,), jnp.int32).at[slot_index].set(token_index)[:slot_total]
    filled = jnp.zeros((slot_total + 1,), jnp.bool_).at[slot_index].set(True)[:slot_total]
    send_rows = jnp.where(filled[:, None], tokens[source], jnp.zeros((), jnp.bfloat16))
    send_rows = send_rows.reshape(groups, per_device, capacity, feature_width)
    gathered = (
        lax.all_gather(w_gate, "dp", axis=1, tiled=True),
        lax.all_gather(w_up, "dp", axis=1, tiled=True),
        lax.all_gather(w_down, "dp", axis=1, tiled=True),
    )
    produced = expert_products(
        lax.all_to_all(send_rows, "expert", split_axis=0, concat_axis=0, tiled=True),
        gathered[0],
        gathered[1],
        gathered[2],
    ).astype(jnp.bfloat16)
    returned = lax.all_to_all(produced, "expert", split_axis=0, concat_axis=0, tiled=True)
    flat_out = returned.reshape(slot_total, feature_width)
    fetched = flat_out[jnp.minimum(slot_index, slot_total - 1)]
    entry_weight = jnp.where(kept_mask, route_weight.reshape(-1), jnp.float32(0.0))
    weighted = fetched.astype(jnp.float32) * entry_weight[:, None]
    mixed = jnp.sum(weighted.reshape(tok_rows, top_count, feature_width), axis=1).astype(
        jnp.bfloat16
    )
    counts_float = local_counts.astype(jnp.float32)
    mean_load = tok_rows * top_count * lax.axis_size("dp") * groups
    totals = lax.psum(counts_float, ("dp", "expert"))
    new_bias = bias + bias_rate * jnp.sign(mean_load - experts * totals)
    return (mixed, new_bias, totals.astype(jnp.int32))


def solution(mesh):
    placed = (
        P(("dp", "expert"), None),
        P(("dp", "expert"), None),
        P(("dp", "expert"), None),
        P(),
        P("expert", "dp", None),
        P("expert", "dp", None),
        P("expert", "dp", None),
    )
    return jax.shard_map(
        body,
        mesh=mesh,
        in_specs=placed,
        out_specs=(P(("dp", "expert"), None), P(), P()),
        check_vma=False,
    )
```

profile of v0, /device:TPU:0, one launch (start us, length us, event | category | flops | bytes accessed | tf_op | source)
XLA Modules:
  0.0 414.9 jit_solution(9385914265346908510)
XLA Ops:
  7.2 0.0 copy-start
  7.2 0.0 all-gather.6.cloned.1.call-start
  7.2 0.7 all-gather.6.cloned.1.call-update
  7.9 0.0 all-gather.4.cloned.1.call-start
  8.0 0.7 all-gather.4.cloned.1.call-update
  8.7 0.8 copy.22
  9.5 0.1 eq.29
  9.5 0.1 eq.25
  9.7 4.5 %reduce-window.6 = s32[16,8,128]{2,1,0:T(8,128)S(1)} reduce-window(s32[16,8,128]{2,1,0:T(8,128)S(1)} %fusion.21, s32[]{:T(128)} %constant.14.clone.1), window={size=1x1x128 pad=0_0x0_0x127_0}, to_apply=%region_0.0 | reduce-window | flops 2080768 | bytes 131076 | tf_op jit(solution)/shard_map/reduce-window
  14.2 0.1 slice.20
  14.2 0.1 copy.24
  14.4 0.1 copy.25
  14.5 0.7 broadcast_multiply_fusion
  15.2 0.1 copy.26
  15.3 0.1 mul.44
  15.4 0.1 broadcast_add_fusion
  15.5 0.1 convert_reduce_fusion
  15.7 4.3 %scatter_custom_fusion.1 = s32[1281]{0:T(1024)S(1)} fusion(s32[1024]{0:T(1024)S(1)} %bitcast.76, s32[1024]{0:T(1024)S(1)} %add_select_fusion, s32[]{:T(128)} %constant.14.clone.1), kind=kCustom, calls=%fused_computation.44 | custom fusion | bytes 5128 | tf_op jit(solution)/shard_map/scatter | solution.py:33
  20.0 4.3 %scatter_custom_fusion = pred[1281]{0:T(1024)(128)(4,1)S(1)} fusion(s32[1024]{0:T(1024)S(1)} %bitcast.77, pred[1024]{0:T(1024)(128)(4,1)S(1)} %broadcast.142, pred[]{:T(512)} %constant.18.clone.1), kind=kCustom, calls=%fused_computation.47 | custom fusion | bytes 1282 | tf_op jit(solution)/shard_map/scatter | solution.py:34
  24.3 0.1 broadcast_in_dim.43
  24.5 0.0 copy-done
  24.5 6.2 %gather_fusion = bf16[1280,2048]{1,0:T(8,128)(2,1)} fusion(bf16[128,2048]{1,0:T(8,128)(2,1)S(1)} %copy-done, s32[2048]{0:T(1024)S(1)} %pad_clamp_fusion), kind=kCustom, calls=%fused_computation | custom fusion | bytes 10490880 | tf_op jit(solution)/shard_map/gather | solution.py:35
  30.7 5.2 %broadcast_select_fusion = bf16[8,2,80,2048]{3,2,1,0:T(8,128)(2,1)} fusion(bf16[8,2,80,2048]{3,2,1,0:T(8,128)(2,1)} %bitcast.70, pred[8,2,80]{2,1,0:T(4,128)(4,1)S(1)} %broadcast_in_dim.43), kind=kLoop, calls=%fused_computation.13 | loop fusion | flops 2621440 | bytes 10487040 | tf_op jit(solution)/shard_map/jit(_where)/select_n | solution.py:35
  35.9 6.4 %all-to-all-start = ((bf16[8,2,80,2048]{3,2,1,0:T(8,128)(2,1)}), bf16[8,2,80,2048]{3,2,1,0:T(8,128)(2,1)}, u32[]{:S(2)}, u32[]{:S(2)}) async-start(bf16[8,2,80,2048]{3,2,1,0:T(8,128)(2,1)} %broadcast_select_fusion), calls=%async_computation | async-start | bytes 10485760 | tf_op jit(solution)/shard_map/all_to_all | solution.py:43
  42.2 0.2 all-gather.8.cloned.1.call-start
  42.5 0.5 all-gather.8.cloned.1.call-update
  43.0 115.8 %all-to-all-done = bf16[8,2,80,2048]{3,2,1,0:T(8,128)(2,1)} async-done(((bf16[8,2,80,2048]{3,2,1,0:T(8,128)(2,1)}), bf16[8,2,80,2048]{3,2,1,0:T(8,128)(2,1)}, u32[]{:S(2)}, u32[]{:S(2)}) %all-to-all-start) | async-done | bytes 5242912 | tf_op jit(solution)/shard_map/all_to_all | solution.py:43
  158.8 0.0 all-gather.6.cloned.1.call-done
  158.8 10.7 %fusion.3 = f32[2,8,80,768]{3,2,1,0:T(8,128)} fusion(bf16[2,768,2048]{2,1,0:T(8,128)(2,1)} %all-gather.6.cloned.1.call-done, bf16[8,2,80,2048]{3,2,1,0:T(8,128)(2,1)} %all-to-all-done), kind=kOutput, calls=%fused_computation.8 | convolution fusion | flops 4026531840 | bytes 15466496 | tf_op jit(solution)/shard_map/sjcd,jfd->sjcf/dot_general | solution.py:11
  169.5 0.0 all-gather.4.cloned.1.call-done
  169.5 56.9 %all-gather.8.cloned.1.call-done = bf16[2,768,2048]{2,1,0:T(8,128)(2,1)} async-done(((bf16[2,192,2048]{2,1,0:T(8,128)(2,1)}), bf16[2,768,2048]{2,1,0:T(8,128)(2,1)}) %all-gather.8.cloned.1.call-update) | async-done | bytes 6291472 | tf_op jit(solution)/shard_map/all_gather | solution.py:40
  226.5 15.6 %convert_bitcast_fusion = bf16[8,2,80,2048]{3,2,0,1:T(8,128)(2,1)} fusion(bf16[2,768,2048]{2,1,0:T(8,128)(2,1)} %all-gather.8.cloned.1.call-done, f32[2,8,80,768]{3,2,1,0:T(8,128)} %fusion.3, bf16[2,768,2048]{2,1,0:T(8,128)(2,1)} %all-gather.4.cloned.1.call-done, bf16[8,2,80,2048]{3,2,1,0:T(8,128)(2,1)} %all-to-all-done), kind=kOutput, calls=%fused_computation.12 | convolution fusion | flops 8061583360 | bytes 27000832 | tf_op jit(solution)/shard_map/sjcf,jfd->sjcd/dot_general | solution.py:13
  242.1 5.6 %copy.29 = bf16[8,2,80,2048]{3,2,1,0:T(8,128)(2,1)} copy(bf16[8,2,80,2048]{3,2,0,1:T(8,128)(2,1)} %convert_bitcast_fusion) | data formatting | bytes 10485760 | tf_op jit(solution)/shard_map/convert_element_type | solution.py:47
  247.7 0.0 copy-start.1
  247.7 0.0 copy-start.2
  247.7 4.8 %all-to-all-start.1 = ((bf16[8,2,80,2048]{3,2,1,0:T(8,128)(2,1)}), bf16[8,2,80,2048]{3,2,1,0:T(8,128)(2,1)}, u32[]{:S(2)}, u32[]{:S(2)}) async-start(bf16[8,2,80,2048]{3,2,1,0:T(8,128)(2,1)} %copy.29), calls=%async_computation.1 | async-start | bytes 10485760 | tf_op jit(solution)/shard_map/all_to_all | solution.py:48
  252.5 135.7 %psum.7 = f32[16]{0:T(128)S(1)} all-reduce(f32[16]{0:T(128)S(1)} %convert_element_type.40), channel_id=1, replica_groups=mesh['dp'=4,'expert'=8] {'dp','expert'}, use_global_device_ids=true, to_apply=%region_7.8 | all-reduce | flops 16 | bytes 128 | tf_op jit(solution)/shard_map/psum | solution.py:58
  388.2 0.1 lt.55
  388.3 0.0 copy-done.1
  388.3 0.1 copy.30
  388.4 0.0 copy-done.2
  388.4 0.5 fusion.29
  389.0 0.0 all-to-all-done.1
  389.0 12.1 %gather_fusion.1 = bf16[1024,2048]{1,0:T(8,128)(2,1)} fusion(bf16[1280,2048]{1,0:T(8,128)(2,1)} %bitcast.14, s32[1024]{0:T(1024)S(1)} %broadcast_clamp_fusion), kind=kCustom, calls=%fused_computation.1 | custom fusion | bytes 8392704 | tf_op jit(solution)/shard_map/gather | solution.py:50
  401.0 7.3 %fusion = bf16[128,2048]{1,0:T(8,128)(2,1)} fusion(bf16[1024,2048]{1,0:T(8,128)(2,1)} %gather_fusion.1, f32[128,8]{1,0:T(8,128)S(1)} %broadcast_select_fusion.1), kind=kLoop, calls=%fused_computation.5 | loop fusion | flops 6029312 | bytes 4722688 | tf_op jit(solution)/shard_map/reduce_sum | solution.py:53
  (13 shorter events, 0.1 us)
Async XLA Ops:
  7.2 17.3 %copy-start = (bf16[128,2048]{1,0:T(8,128)(2,1)S(1)}, bf16[128,2048]{1,0:T(8,128)(2,1)}, u32[]{:S(2)}) copy-start(bf16[128,2048]{1,0:T(8,128)(2,1)} %param.7) | copy-start | bytes 1572868
  7.2 151.6 %all-gather.6.cloned.1.call-start = ((), (), s32[]{:S(2)}) async-start(), calls=%async_computation.3 | async-start | bytes 7864320 | tf_op jit(solution)/shard_map/all_gather | solution.py:39
  7.9 161.6 %all-gather.4.cloned.1.call-start = ((), (), s32[]{:S(2)}) async-start(), calls=%async_computation.2 | async-start | bytes 7864320 | tf_op jit(solution)/shard_map/all_gather | solution.py:38
  35.9 122.9 %all-to-all-start = ((bf16[8,2,80,2048]{3,2,1,0:T(8,128)(2,1)}), bf16[8,2,80,2048]{3,2,1,0:T(8,128)(2,1)}, u32[]{:S(2)}, u32[]{:S(2)}) async-start(bf16[8,2,80,2048]{3,2,1,0:T(8,128)(2,1)} %broadcast_select_fusion), calls=%async_computation | async-start | bytes 10485760 | tf_op jit(solution)/shard_map/all_to_all | solution.py:43
  42.2 184.2 %all-gather.8.cloned.1.call-start = ((), (), s32[]{:S(2)}) async-start(), calls=%async_computation.4 | async-start | bytes 7864320 | tf_op jit(solution)/shard_map/all_gather | solution.py:40
  247.7 140.6 %copy-start.1 = (f32[128,8]{0,1:T(8,128)S(1)}, f32[128,8]{0,1:T(8,128)}, u32[]{:S(2)}) copy-start(f32[128,8]{0,1:T(8,128)} %param.9) | copy-start | bytes 12292
  247.7 140.8 %copy-start.2 = (f32[16]{0:T(128)S(1)}, f32[16]{0:T(128)}, u32[]{:S(2)}) copy-start(f32[16]{0:T(128)} %param.10) | copy-start | bytes 196
  247.7 141.3 %all-to-all-start.1 = ((bf16[8,2,80,2048]{3,2,1,0:T(8,128)(2,1)}), bf16[8,2,80,2048]{3,2,1,0:T(8,128)(2,1)}, u32[]{:S(2)}, u32[]{:S(2)}) async-start(bf16[8,2,80,2048]{3,2,1,0:T(8,128)(2,1)} %copy.29), calls=%async_computation.1 | async-start | bytes 10485760 | tf_op jit(solution)/shard_map/all_to_all | solution.py:48
Sparse Core Ops, SparseCore 0:
  9.8 72.7 all-gather.5
  84.5 70.0 all-gather.3
  156.4 70.0 all-gather.7
where the time goes:
time: 415 us
  waiting for transfers between devices  175 us (42%)
  blocking collectives  136 us (33%)
  local copies, waits for them, and re-layouts  34.3 us (8%)
  matrix products  26.3 us (6%)
  other arithmetic  18.6 us (4%)
  between operations  13.9 us (3%)
  starting transfers between devices  11.4 us (3%)
    psum x1, blocking collectives, body(): totals = lax.psum(counts_float, ('dp', 'expert'))  136 us
    all_to_all x1, waiting for transfers between devices, body(): lax.all_to_all(send_rows, 'expert', split_axis=0, concat_axis=0, tiled=True)  116 us
    all_gather x1, waiting for transfers between devices, body(): lax.all_gather(w_down, 'dp', axis=1, tiled=True)  56.9 us
    dot_general x1, matrix products, expert_products(): jnp.einsum('sjcf,jfd->sjcd', hidden, down_w, preferred_element_type=jnp.f...  15.6 us
    gather x1, local copies, waits for them, and re-layouts, body(): fetched = flat_out[jnp.minimum(slot_index, slot_total - 1)]  12.1 us
    dot_general x1, matrix products, expert_products(): jnp.einsum('sjcd,jfd->sjcf', received, up_w, preferred_element_type=jnp.f...  10.7 us
  transfers between devices with their start and end apart: 5, of which 2 were waited for; matrix products, arithmetic and copies ran while one was open for 9% of the time, Pallas kernels for 0%

commit v1 on v0

--- a/solution.py
+++ b/solution.py
@@ -1,9 +1,16 @@
+import functools
+
 import jax
 import jax.numpy as jnp
 from jax import lax
+from jax.experimental import pallas as pl
+from jax.experimental.pallas import tpu as pltpu
 from jax.sharding import PartitionSpec as P
 
 bias_rate = 0.05
+MESH = pl.DeviceIdType.MESH
+VMEM_BYTES = 67043328
+chunks = 4
 
 
 def expert_products(received, gate_w, up_w, down_w):
@@ -13,7 +20,7 @@
     return jnp.einsum("sjcf,jfd->sjcd", hidden, down_w, preferred_element_type=jnp.float32)
 
 
-def body(tokens, routes, route_weight, bias, w_gate, w_up, w_down):
+def exchange_body(tokens, routes, route_weight, bias, w_gate, w_up, w_down):
     tok_rows, feature_width = tokens.shape
     top_count = routes.shape[1]
     experts = bias.shape[0]
@@ -34,16 +41,9 @@
     filled = jnp.zeros((slot_total + 1,), jnp.bool_).at[slot_index].set(True)[:slot_total]
     send_rows = jnp.where(filled[:, None], tokens[source], jnp.zeros((), jnp.bfloat16))
     send_rows = send_rows.reshape(groups, per_device, capacity, feature_width)
-    gathered = (
-        lax.all_gather(w_gate, "dp", axis=1, tiled=True),
-        lax.all_gather(w_up, "dp", axis=1, tiled=True),
-        lax.all_gather(w_down, "dp", axis=1, tiled=True),
-    )
+    gathered = [lax.all_gather(w, "dp", axis=1, tiled=True) for w in (w_gate, w_up, w_down)]
     produced = expert_products(
-        lax.all_to_all(send_rows, "expert", split_axis=0, concat_axis=0, tiled=True),
-        gathered[0],
-        gathered[1],
-        gathered[2],
+        lax.all_to_all(send_rows, "expert", split_axis=0, concat_axis=0, tiled=True), *gathered
     ).astype(jnp.bfloat16)
     returned = lax.all_to_all(produced, "expert", split_axis=0, concat_axis=0, tiled=True)
     flat_out = returned.reshape(slot_total, feature_width)
@@ -53,11 +53,342 @@
     mixed = jnp.sum(weighted.reshape(tok_rows, top_count, feature_width), axis=1).astype(
         jnp.bfloat16
     )
-    counts_float = local_counts.astype(jnp.float32)
     mean_load = tok_rows * top_count * lax.axis_size("dp") * groups
-    totals = lax.psum(counts_float, ("dp", "expert"))
+    totals = lax.psum(local_counts.astype(jnp.float32), ("dp", "expert"))
     new_bias = bias + bias_rate * jnp.sign(mean_load - experts * totals)
     return (mixed, new_bias, totals.astype(jnp.int32))
+
+
+def layer_kernel(
+    zs, capacity, per_device,
+    tokens, routes_t, weights_t, w_gate, w_up, w_down,
+    out, totals,
+    tok, table, gate_w, up_w, down_own, down_far, hidden,
+    part1, recv1, part2, recv2, part3, recv3, tally, tally_in,
+    tok_in, tok_out, tab_in, tab_out, own_sem, w_in, w_out, d_in, d_out,
+    s1_in, s1_out, s2_in, s2_out, s3_in, s3_out, t_in, t_out,
+):
+    rows, width = tokens.shape
+    top = routes_t.shape[0]
+    experts = table.shape[1] // 2
+    ff = w_gate.shape[0]
+    unit = ff // per_device
+    cd = width // chunks
+    slots = tok.shape[0]
+    dp, ex = lax.axis_index("dp"), lax.axis_index("expert")
+    y, x = dp // 2, dp % 2
+    z, c = ex // 2, ex % 2
+
+    def at(y_, x_, z_, c_):
+        return (y_ * 2 + x_, z_ * 2 + c_)
+
+    def slot(y_, z_, c_):
+        return (y_ * zs + z_) * 2 + c_
+
+    def far(step):
+        return lax.rem(z + step, zs)
+
+    mate = at(y, x, z, 1 - c)
+    y_side = at(1 - y, x, z, c)
+    x_side = at(y, 1 - x, z, c)
+    me = slot(y, z, c)
+
+    barrier = pltpu.get_barrier_semaphore()
+    partners = [mate, y_side, x_side] + [at(y, x, far(s), c) for s in range(1, zs)]
+    for partner in partners:
+        pl.semaphore_signal(barrier, inc=1, device_id=partner, device_id_type=MESH)
+
+    own = [
+        pltpu.make_async_copy(tokens, tok.at[me], own_sem.at[0]),
+        pltpu.make_async_copy(w_gate, gate_w.at[0], own_sem.at[1]),
+        pltpu.make_async_copy(w_up, up_w.at[0], own_sem.at[2]),
+        pltpu.make_async_copy(w_down, down_own, own_sem.at[3]),
+    ]
+    for copy in own:
+        copy.start()
+
+    labels = lax.broadcasted_iota(jnp.int32, (experts, rows), 0)
+    picked = jnp.zeros((experts, rows), jnp.float32)
+    weight = jnp.zeros((experts, rows), jnp.float32)
+    for k in range(top):
+        same = labels == routes_t[k : k + 1, :]
+        picked += jnp.where(same, 1.0, 0.0)
+        weight += jnp.where(same, weights_t[k : k + 1, :], 0.0)
+    earlier = jnp.where(
+        lax.broadcasted_iota(jnp.int32, (rows, rows), 0)
+        < lax.broadcasted_iota(jnp.int32, (rows, rows), 1),
+        1.0,
+        0.0,
+    )
+    rank = jnp.dot(
+        picked.astype(jnp.bfloat16),
+        earlier.astype(jnp.bfloat16),
+        preferred_element_type=jnp.float32,
+    )
+    table[me, 0:experts, :] = jnp.where(rank < capacity, weight, 0.0)
+    table[me, experts : 2 * experts, :] = picked
+
+    pl.semaphore_wait(barrier, len(partners))
+
+    sent = []
+
+    def remote(src, dst, ssem, rsem, device):
+        copy = pltpu.make_async_remote_copy(
+            src_ref=src, dst_ref=dst, send_sem=ssem, recv_sem=rsem,
+            device_id=device, device_id_type=MESH,
+        )
+        copy.start()
+        sent.append(copy)
+
+    def landed(ref, sem):
+        pltpu.make_async_copy(ref, ref, sem).wait()
+
+    order = [0]
+
+    def pass_on(index, device, first=False):
+        n = order[0]
+        order[0] += 1
+        remote(table.at[index], table.at[index], tab_out.at[n], tab_in.at[index], device)
+        remote(
+            tokens if first else tok.at[index], tok.at[index],
+            tok_out.at[n], tok_in.at[index], device,
+        )
+
+    def arrived(index):
+        landed(table.at[index], tab_in.at[index])
+        landed(tok.at[index], tok_in.at[index])
+
+    remote(w_gate, gate_w.at[1], w_out.at[0], w_in.at[0], x_side)
+    remote(w_up, up_w.at[1], w_out.at[1], w_in.at[1], x_side)
+    pass_on(me, y_side, True)
+    for s in range(1, zs):
+        pass_on(me, at(y, x, far(s), c), True)
+    pass_on(me, mate, True)
+    for j in range(chunks):
+        remote(
+            w_down.at[:, j * cd : (j + 1) * cd], down_far.at[j], d_out.at[j], d_in.at[j], x_side
+        )
+    for copy in own:
+        copy.wait()
+
+    def scales(index):
+        columns = []
+        for j in range(per_device):
+            row = table[index, pl.ds(ex * per_device + j, 1), :]
+            columns.append(jnp.transpose(jnp.broadcast_to(row, (rows, rows))))
+        lanes = columns[0].shape[1]
+        place = lax.broadcasted_iota(jnp.int32, (rows, lanes), 1)
+        pieces = []
+        for t in range(ff // lanes):
+            piece = columns[0]
+            for j in range(1, per_device):
+                piece = jnp.where(place + t * lanes >= j * unit, columns[j], piece)
+            pieces.append(piece)
+        return jnp.concatenate(pieces, axis=1)
+
+    nt = (((1,), (1,)), ((), ()))
+
+    def hide(first, count, half):
+        block = tok[pl.ds(first, count)].reshape(count * rows, width)
+        gate = lax.dot_general(block, gate_w[half], nt, preferred_element_type=jnp.float32)
+        up = lax.dot_general(block, up_w[half], nt, preferred_element_type=jnp.float32)
+        act = gate / (1.0 + jnp.exp(-gate)) * up
+        for i in range(count):
+            value = act[i * rows : (i + 1) * rows] * scales(first + i)
+            hidden[first + i, :, half * ff : (half + 1) * ff] = value.astype(jnp.bfloat16)
+
+    def pair(y_, z_):
+        arrived(slot(y_, z_, 1 - c))
+        hide(slot(y_, z_, 0), 2, 0)
+
+    arrived(slot(1 - y, z, c))
+    pass_on(slot(1 - y, z, c), mate)
+    for s in range(1, zs):
+        from_z = lax.rem(z + zs - s, zs)
+        arrived(slot(y, from_z, c))
+        pass_on(slot(y, from_z, c), y_side)
+        pass_on(slot(y, from_z, c), mate)
+        if s == 1:
+            pair(y, z)
+            pair(1 - y, z)
+        else:
+            pair(y, lax.rem(z + zs - s + 1, zs))
+    pair(y, lax.rem(z + 1, zs))
+    for s in range(1, zs):
+        from_z = lax.rem(z + zs - s, zs)
+        arrived(slot(1 - y, from_z, c))
+        pass_on(slot(1 - y, from_z, c), mate)
+        if s > 1:
+            pair(1 - y, lax.rem(z + zs - s + 1, zs))
+    pair(1 - y, lax.rem(z + 1, zs))
+
+    def add_tally(i, total):
+        return total + table[i, experts : 2 * experts, :]
+
+    tally[...] = lax.fori_loop(0, slots, add_tally, jnp.zeros((experts, rows), jnp.float32))
+
+    landed(gate_w.at[1], w_in.at[0])
+    landed(up_w.at[1], w_in.at[1])
+    remote(tally, tally_in, t_out, t_in, x_side)
+
+    batch = 4
+
+    def other_half(q, carry):
+        hide(q * batch, batch, 1)
+        return carry
+
+    lax.fori_loop(0, slots // batch, other_half, 0)
+
+    def down(j):
+        landed(down_far.at[j], d_in.at[j])
+
+        def step(q, carry):
+            near = hidden[pl.ds(q * batch, batch)].reshape(batch * rows, 2 * ff)
+            value = jnp.dot(
+                near[:, :ff], down_own[:, j * cd : (j + 1) * cd],
+                preferred_element_type=jnp.float32,
+            ) + jnp.dot(near[:, ff:], down_far[j], preferred_element_type=jnp.float32)
+            value = value.astype(jnp.bfloat16)
+            for i in range(batch):
+                part1[j, i % 2, q * (batch // 2) + i // 2] = value[i * rows : (i + 1) * rows]
+            return carry
+
+        lax.fori_loop(0, slots // batch, step, 0)
+        remote(part1.at[j, 1 - c], recv1.at[j], s1_out.at[j], s1_in.at[j], mate)
+
+    def over_core(j):
+        landed(recv1.at[j], s1_in.at[j])
+
+        def step(i, carry):
+            value = part1[j, c, i].astype(jnp.float32) + recv1[j, i].astype(jnp.float32)
+            part2[j, i] = value.astype(jnp.bfloat16)
+            return carry
+
+        lax.fori_loop(0, slots // 2, step, 0)
+        remote(
+            part2.at[j, pl.ds((1 - y) * zs, zs)], recv2.at[j], s2_out.at[j], s2_in.at[j], y_side
+        )
+
+    def over_y(j):
+        landed(recv2.at[j], s2_in.at[j])
+
+        def step(i, carry):
+            value = part2[j, y * zs + i].astype(jnp.float32) + recv2[j, i].astype(jnp.float32)
+            part3[j, i] = value.astype(jnp.bfloat16)
+            return carry
+
+        lax.fori_loop(0, zs, step, 0)
+        for s in range(1, zs):
+            remote(
+                part3.at[j, far(s)], recv3.at[j, s - 1],
+                s3_out.at[j, s - 1], s3_in.at[j, s - 1], at(y, x, far(s), c),
+            )
+
+    def over_z(j):
+        value = part3[j, z].astype(jnp.float32)
+        for s in range(1, zs):
+            landed(recv3.at[j, s - 1], s3_in.at[j, s - 1])
+            value += recv3[j, s - 1].astype(jnp.float32)
+        out[:, j * cd : (j + 1) * cd] = value.astype(jnp.bfloat16)
+
+    for j in range(chunks + 3):
+        if j < chunks:
+            down(j)
+        if 0 <= j - 1 < chunks:
+            over_core(j - 1)
+        if 0 <= j - 2 < chunks:
+            over_y(j - 2)
+        if 0 <= j - 3 < chunks:
+            over_z(j - 3)
+
+    landed(tally_in, t_in)
+    count = jnp.sum(tally[...] + tally_in[...], axis=1, keepdims=True)
+    totals[...] = jnp.broadcast_to(count, totals.shape)
+    for copy in sent:
+        copy.wait_send()
+
+
+def group_scratch(zs, rows, width, ff, experts):
+    slots = 4 * zs
+    cd = width // chunks
+    bf, f32 = jnp.bfloat16, jnp.float32
+    return [
+        ((slots, rows, width), bf),
+        ((slots, 2 * experts, rows), f32),
+        ((2, ff, width), bf),
+        ((2, ff, width), bf),
+        ((ff, width), bf),
+        ((chunks, ff, cd), bf),
+        ((slots, rows, 2 * ff), bf),
+        ((chunks, 2, slots // 2, rows, cd), bf),
+        ((chunks, slots // 2, rows, cd), bf),
+        ((chunks, slots // 2, rows, cd), bf),
+        ((chunks, zs, rows, cd), bf),
+        ((chunks, zs, rows, cd), bf),
+        ((chunks, zs - 1, rows, cd), bf),
+        ((experts, rows), f32),
+        ((experts, rows), f32),
+    ]
+
+
+def group_body(zs, tokens, routes, route_weight, bias, w_gate, w_up, w_down):
+    rows, width = tokens.shape
+    experts = bias.shape[0]
+    per_device, unit, _ = w_gate.shape
+    ff = per_device * unit
+    top = routes.shape[1]
+    capacity = 5 * rows * top // (4 * experts)
+    slots = 4 * zs
+    dma = pltpu.SemaphoreType.DMA
+    vmem = pl.BlockSpec(memory_space=pltpu.VMEM)
+    anywhere = pl.BlockSpec(memory_space=pl.ANY)
+    mixed, totals = pl.pallas_call(
+        functools.partial(layer_kernel, zs, capacity, per_device),
+        out_shape=(
+            jax.ShapeDtypeStruct((rows, width), jnp.bfloat16),
+            jax.ShapeDtypeStruct((experts, rows), jnp.float32),
+        ),
+        in_specs=[anywhere, vmem, vmem, anywhere, anywhere, anywhere],
+        out_specs=(vmem, vmem),
+        scratch_shapes=[
+            pltpu.VMEM(shape, kind)
+            for shape, kind in group_scratch(zs, rows, width, ff, experts)
+        ]
+        + [
+            dma((slots,)), dma((slots,)), dma((slots,)), dma((slots,)), dma((4,)),
+            dma((2,)), dma((2,)), dma((chunks,)), dma((chunks,)),
+            dma((chunks,)), dma((chunks,)), dma((chunks,)), dma((chunks,)),
+            dma((chunks, zs - 1)), dma((chunks, zs - 1)), dma, dma,
+        ],
+        compiler_params=pltpu.CompilerParams(
+            collective_id=0, has_side_effects=True, vmem_limit_bytes=VMEM_BYTES
+        ),
+    )(
+        tokens, routes.T, route_weight.T,
+        w_gate.reshape(ff, width), w_up.reshape(ff, width), w_down.reshape(ff, width),
+    )
+    counts = totals[:, 0]
+    mean_load = rows * top * lax.axis_size("dp") * lax.axis_size("expert")
+    new_bias = bias + bias_rate * jnp.sign(mean_load - experts * counts)
+    return (mixed, new_bias, counts.astype(jnp.int32))
+
+
+def body(tokens, routes, route_weight, bias, w_gate, w_up, w_down):
+    rows, width = tokens.shape
+    per_device, unit, _ = w_gate.shape
+    groups = lax.axis_size("expert")
+    zs = groups // 2
+    held = group_scratch(zs, rows, width, per_device * unit, bias.shape[0])
+    total = 0
+    for shape, kind in held:
+        size = jnp.dtype(kind).itemsize
+        for extent in shape:
+            size *= extent
+        total += size
+    args = (tokens, routes, route_weight, bias, w_gate, w_up, w_down)
+    if lax.axis_size("dp") == 4 and groups % 2 == 0 and zs > 1 and total < 0.85 * VMEM_BYTES:
+        return group_body(zs, *args)
+    return exchange_body(*args)
 
 
 def solution(mesh):

time: 415 us -> 162 us (0.39)
  waiting for transfers between devices: 175 us -> 0 us
  Pallas kernels: 0 us -> 156 us
  blocking collectives: 136 us -> 0 us
  local copies, waits for them, and re-layouts: 34.3 us -> 1.88 us
  matrix products: 26.3 us -> 0 us
  other arithmetic: 18.6 us -> 3.31 us
  between operations: 13.9 us -> 0.64 us
  starting transfers between devices: 11.4 us -> 0 us
    pallas_call x0 -> x1, Pallas kernels: none -> 156 us  [group_body(): pl.pallas_call(functools.partial(layer_kernel, zs, capacity, per_device),...]
    psum x1 -> x0, blocking collectives: 136 us -> none  [body(): totals = lax.psum(counts_float, ('dp', 'expert'))]
    all_to_all x2 -> x0, waiting for transfers between devices: 116 us -> none  [the longest x1 116 us: body(): lax.all_to_all(send_rows, 'expert', split_axis=0, concat_axis=0, tiled=True)]
    all_gather x3 -> x0, waiting for transfers between devices: 56.9 us -> none  [the longest x1 56.9 us: body(): lax.all_gather(w_down, 'dp', axis=1, tiled=True)]
    dot_general x2 -> x0, matrix products: 26.3 us -> none  [the longest x1 15.6 us: expert_products(): jnp.einsum('sjcf,jfd->sjcd', hidden, down_w, preferred_element_type=jnp.f...]
    gather x2 -> x0, local copies, waits for them, and re-layouts: 18.2 us -> none  [the longest x1 12.1 us: body(): fetched = flat_out[jnp.minimum(slot_index, slot_total - 1)]]
    all_to_all x2 -> x0, starting transfers between devices: 11.1 us -> none  [the longest x1 6.35 us: body(): lax.all_to_all(send_rows, 'expert', split_axis=0, concat_axis=0, tiled=True)]
    scatter x2 -> x0, local copies, waits for them, and re-layouts: 8.66 us -> none  [the longest x1 4.34 us: body(): jnp.zeros((slot_total + 1,), jnp.bool_).at[slot_index].set(True)]
  transfers between devices with their start and end apart: 5 -> 0, of which waited for: 2 -> 0; matrix products, arithmetic and copies ran while one was open for 9% -> 0% of each run, Pallas kernels for 0% -> 0%
where the time goes in v1:
time: 162 us; the launch traced here: 161 us
  Pallas kernels  156 us (96%)
  other arithmetic  3.31 us (2%)
  local copies, waits for them, and re-layouts  1.88 us (1%)
    pallas_call x1, Pallas kernels, group_body(): pl.pallas_call(functools.partial(layer_kernel, zs, capacity, per_device),...  156 us

profile of v1, /device:TPU:0, one launch (start us, length us, event | category | flops | bytes accessed | tf_op | source)
XLA Modules:
  0.0 161.5 jit_solution(7424521908756545640)
XLA Ops:
  0.6 155.7 %shard_map.94 = (bf16[128,2048]{1,0:T(8,128)(2,1)}, f32[16,128]{1,0:T(8,128)}) custom-call(bf16[128,2048]{1,0:T(8,128)(2,1)} %tokens.1, s32[8,128]{1,0:T(8,128)} %bitcast.8, f32[8,128]{1,0:T(8,128)} %bitcast.9, bf16[384,2048]{1,0:T(8,128)(2,1)} %bitcast.5, bf16[384,2048]{1,0:T(8,128)(2,1)} %bitcast.6, bf16[384,2048]{1,0:T(8,128)(2,1)} %bitcast.7), custom_call_target="tpu_custom_call" | custom-call | tf_op jit(solution)/shard_map/pallas_call | solution.py:345
  156.3 0.8 multiply_reduce_fusion
  157.1 1.2 add.3
  158.3 1.3 convert_reduce_fusion
  159.6 1.9 %copy.11 = bf16[128,2048]{1,0:T(8,128)(2,1)} copy(bf16[128,2048]{1,0:T(8,128)(2,1)} %get-tuple-element.10) | data formatting | bytes 1048576

commit v2 on v1

--- a/solution.py
+++ b/solution.py
@@ -10,7 +10,7 @@
 bias_rate = 0.05
 MESH = pl.DeviceIdType.MESH
 VMEM_BYTES = 67043328
-chunks = 4
+chunks = 8
 
 
 def expert_products(received, gate_w, up_w, down_w):
@@ -64,7 +64,7 @@
     tokens, routes_t, weights_t, w_gate, w_up, w_down,
     out, totals,
     tok, table, gate_w, up_w, down_own, down_far, hidden,
-    part1, recv1, part2, recv2, part3, recv3, tally, tally_in,
+    part1, keep1, recv1, part2, keep2, recv2, part3, keep3, recv3, tally, tally_in,
     tok_in, tok_out, tab_in, tab_out, own_sem, w_in, w_out, d_in, d_out,
     s1_in, s1_out, s2_in, s2_out, s3_in, s3_out, t_in, t_out,
 ):
@@ -132,38 +132,50 @@
 
     sent = []
 
-    def remote(src, dst, ssem, rsem, device):
+    def remote(src, dst, ssem, rsem, device, keep=True):
         copy = pltpu.make_async_remote_copy(
             src_ref=src, dst_ref=dst, send_sem=ssem, recv_sem=rsem,
             device_id=device, device_id_type=MESH,
         )
         copy.start()
-        sent.append(copy)
+        if keep:
+            sent.append(copy)
 
     def landed(ref, sem):
         pltpu.make_async_copy(ref, ref, sem).wait()
 
-    order = [0]
-
-    def pass_on(index, device, first=False):
-        n = order[0]
-        order[0] += 1
-        remote(table.at[index], table.at[index], tab_out.at[n], tab_in.at[index], device)
+    def pass_on(n, index, device, source=None):
+        remote(table.at[index], table.at[index], tab_out.at[n], tab_in.at[index], device, False)
         remote(
-            tokens if first else tok.at[index], tok.at[index],
-            tok_out.at[n], tok_in.at[index], device,
+            tok.at[index] if source is None else source, tok.at[index],
+            tok_out.at[n], tok_in.at[index], device, False,
         )
+
+    def passed(n):
+        pltpu.make_async_copy(table.at[0], table.at[0], tab_out.at[n]).wait()
+        pltpu.make_async_copy(tok.at[0], tok.at[0], tok_out.at[n]).wait()
 
     def arrived(index):
         landed(table.at[index], tab_in.at[index])
         landed(tok.at[index], tok_in.at[index])
 
-    remote(w_gate, gate_w.at[1], w_out.at[0], w_in.at[0], x_side)
-    remote(w_up, up_w.at[1], w_out.at[1], w_in.at[1], x_side)
-    pass_on(me, y_side, True)
-    for s in range(1, zs):
-        pass_on(me, at(y, x, far(s), c), True)
-    pass_on(me, mate, True)
+    above, below = z < zs - 1, z > 0
+    z_up, z_down = at(y, x, z + 1, c), at(y, x, z - 1, c)
+
+    for j in range(per_device):
+        units = pl.ds(j * unit, unit)
+        remote(w_gate.at[units], gate_w.at[1, units], w_out.at[0, j], w_in.at[0, j], x_side)
+        remote(w_up.at[units], up_w.at[1, units], w_out.at[1, j], w_in.at[1, j], x_side)
+    @pl.when(above)
+    def _():
+        pass_on(z, me, z_up, tokens)
+
+    @pl.when(below)
+    def _():
+        pass_on(zs + z, me, z_down, tokens)
+
+    pass_on(2 * zs + z, me, y_side, tokens)
+    pass_on(3 * zs + me // 2, me, mate, tokens)
     for j in range(chunks):
         remote(
             w_down.at[:, j * cd : (j + 1) * cd], down_far.at[j], d_out.at[j], d_in.at[j], x_side
@@ -171,11 +183,12 @@
     for copy in own:
         copy.wait()
 
+    def column(index, j):
+        row = table[index, pl.ds(ex * per_device + j, 1), :]
+        return jnp.transpose(jnp.broadcast_to(row, (rows, rows)))
+
     def scales(index):
-        columns = []
-        for j in range(per_device):
-            row = table[index, pl.ds(ex * per_device + j, 1), :]
-            columns.append(jnp.transpose(jnp.broadcast_to(row, (rows, rows))))
+        columns = [column(index, j) for j in range(per_device)]
         lanes = columns[0].shape[1]
         place = lax.broadcasted_iota(jnp.int32, (rows, lanes), 1)
         pieces = []
@@ -188,56 +201,91 @@
 
     nt = (((1,), (1,)), ((), ()))
 
-    def hide(first, count, half):
-        block = tok[pl.ds(first, count)].reshape(count * rows, width)
-        gate = lax.dot_general(block, gate_w[half], nt, preferred_element_type=jnp.float32)
-        up = lax.dot_general(block, up_w[half], nt, preferred_element_type=jnp.float32)
-        act = gate / (1.0 + jnp.exp(-gate)) * up
-        for i in range(count):
-            value = act[i * rows : (i + 1) * rows] * scales(first + i)
-            hidden[first + i, :, half * ff : (half + 1) * ff] = value.astype(jnp.bfloat16)
-
-    def pair(y_, z_):
-        arrived(slot(y_, z_, 1 - c))
-        hide(slot(y_, z_, 0), 2, 0)
-
-    arrived(slot(1 - y, z, c))
-    pass_on(slot(1 - y, z, c), mate)
-    for s in range(1, zs):
-        from_z = lax.rem(z + zs - s, zs)
-        arrived(slot(y, from_z, c))
-        pass_on(slot(y, from_z, c), y_side)
-        pass_on(slot(y, from_z, c), mate)
-        if s == 1:
-            pair(y, z)
-            pair(1 - y, z)
-        else:
-            pair(y, lax.rem(z + zs - s + 1, zs))
-    pair(y, lax.rem(z + 1, zs))
-    for s in range(1, zs):
-        from_z = lax.rem(z + zs - s, zs)
-        arrived(slot(1 - y, from_z, c))
-        pass_on(slot(1 - y, from_z, c), mate)
-        if s > 1:
-            pair(1 - y, lax.rem(z + zs - s + 1, zs))
-    pair(1 - y, lax.rem(z + 1, zs))
+    def act(block, gate_t, up_t):
+        gate = lax.dot_general(block, gate_t, nt, preferred_element_type=jnp.float32)
+        up = lax.dot_general(block, up_t, nt, preferred_element_type=jnp.float32)
+        return gate / (1.0 + jnp.exp(-gate)) * up
+
+    batch = 4
+
+    def relay(source, onward, device, n):
+        index = slot(y, source, c)
+        arrived(index)
+
+        @pl.when(onward)
+        def _():
+            pass_on(n + source, index, device)
+
+        pass_on(2 * zs + source, index, y_side)
+        pass_on(3 * zs + index // 2, index, mate)
+
+    for d in range(1, zs):
+
+        @pl.when(z >= d)
+        def _():
+            relay(z - d, above, z_up, 0)
+
+        @pl.when(z + d < zs)
+        def _():
+            relay(z + d, below, z_down, zs)
+
+    def from_y(source):
+        index = slot(1 - y, source, c)
+        arrived(index)
+        pass_on(3 * zs + index // 2, index, mate)
+
+    from_y(z)
+    for d in range(1, zs):
+
+        @pl.when(z >= d)
+        def _():
+            from_y(z - d)
+
+        @pl.when(z + d < zs)
+        def _():
+            from_y(z + d)
+
+    def from_mate(i, carry):
+        arrived(2 * i + 1 - c)
+        return carry
+
+    lax.fori_loop(0, slots // 2, from_mate, 0)
+
+    def own_half(q, carry):
+        first = q * batch
+        block = tok[pl.ds(first, batch)].reshape(batch * rows, width)
+        value = act(block, gate_w[0], up_w[0])
+        for i in range(batch):
+            scaled = value[i * rows : (i + 1) * rows] * scales(first + i)
+            hidden[first + i, :, 0:ff] = scaled.astype(jnp.bfloat16)
+        return carry
+
+    lax.fori_loop(0, slots // batch, own_half, 0)
 
     def add_tally(i, total):
         return total + table[i, experts : 2 * experts, :]
 
     tally[...] = lax.fori_loop(0, slots, add_tally, jnp.zeros((experts, rows), jnp.float32))
 
-    landed(gate_w.at[1], w_in.at[0])
-    landed(up_w.at[1], w_in.at[1])
     remote(tally, tally_in, t_out, t_in, x_side)
 
-    batch = 4
-
-    def other_half(q, carry):
-        hide(q * batch, batch, 1)
-        return carry
-
-    lax.fori_loop(0, slots // batch, other_half, 0)
+    for j in range(per_device):
+        units = pl.ds(j * unit, unit)
+        landed(gate_w.at[1, units], w_in.at[0, j])
+        landed(up_w.at[1, units], w_in.at[1, j])
+
+        def other_half(q, carry):
+            first = q * batch
+            block = tok[pl.ds(first, batch)].reshape(batch * rows, width)
+            value = act(block, gate_w[1, j * unit : (j + 1) * unit], up_w[1, j * unit : (j + 1) * unit])
+            for i in range(batch):
+                scaled = value[i * rows : (i + 1) * rows] * column(first + i, j)[:, 0:1]
+                hidden[first + i, :, ff + j * unit : ff + (j + 1) * unit] = scaled.astype(
+                    jnp.bfloat16
+                )
+            return carry
+
+        lax.fori_loop(0, slots // batch, other_half, 0)
 
     def down(j):
         landed(down_far.at[j], d_in.at[j])
@@ -248,44 +296,50 @@
                 near[:, :ff], down_own[:, j * cd : (j + 1) * cd],
                 preferred_element_type=jnp.float32,
             ) + jnp.dot(near[:, ff:], down_far[j], preferred_element_type=jnp.float32)
-            value = value.astype(jnp.bfloat16)
-            for i in range(batch):
-                part1[j, i % 2, q * (batch // 2) + i // 2] = value[i * rows : (i + 1) * rows]
+            for i in range(batch // 2):
+                one = value[2 * i * rows : (2 * i + 1) * rows]
+                two = value[(2 * i + 1) * rows : (2 * i + 2) * rows]
+                keep1[j, q * (batch // 2) + i] = jnp.where(c == 0, one, two)
+                part1[j, q * (batch // 2) + i] = jnp.where(c == 0, two, one).astype(jnp.bfloat16)
             return carry
 
         lax.fori_loop(0, slots // batch, step, 0)
-        remote(part1.at[j, 1 - c], recv1.at[j], s1_out.at[j], s1_in.at[j], mate)
+        remote(part1.at[j], recv1.at[j], s1_out.at[j], s1_in.at[j], mate)
 
     def over_core(j):
         landed(recv1.at[j], s1_in.at[j])
 
-        def step(i, carry):
-            value = part1[j, c, i].astype(jnp.float32) + recv1[j, i].astype(jnp.float32)
+        def away(i, carry):
+            n = (1 - y) * zs + i
+            value = keep1[j, n] + recv1[j, n].astype(jnp.float32)
             part2[j, i] = value.astype(jnp.bfloat16)
             return carry
 
-        lax.fori_loop(0, slots // 2, step, 0)
-        remote(
-            part2.at[j, pl.ds((1 - y) * zs, zs)], recv2.at[j], s2_out.at[j], s2_in.at[j], y_side
-        )
+        lax.fori_loop(0, zs, away, 0)
+        remote(part2.at[j], recv2.at[j], s2_out.at[j], s2_in.at[j], y_side)
+
+        def home(i, carry):
+            n = y * zs + i
+            keep2[j, i] = keep1[j, n] + recv1[j, n].astype(jnp.float32)
+            return carry
+
+        lax.fori_loop(0, zs, home, 0)
 
     def over_y(j):
         landed(recv2.at[j], s2_in.at[j])
 
-        def step(i, carry):
-            value = part2[j, y * zs + i].astype(jnp.float32) + recv2[j, i].astype(jnp.float32)
-            part3[j, i] = value.astype(jnp.bfloat16)
-            return carry
-
-        lax.fori_loop(0, zs, step, 0)
         for s in range(1, zs):
+            n = far(s)
+            value = keep2[j, n] + recv2[j, n].astype(jnp.float32)
+            part3[j, s - 1] = value.astype(jnp.bfloat16)
             remote(
-                part3.at[j, far(s)], recv3.at[j, s - 1],
-                s3_out.at[j, s - 1], s3_in.at[j, s - 1], at(y, x, far(s), c),
+                part3.at[j, s - 1], recv3.at[j, s - 1],
+                s3_out.at[j, s - 1], s3_in.at[j, s - 1], at(y, x, n, c),
             )
+        keep3[j] = keep2[j, z] + recv2[j, z].astype(jnp.float32)
 
     def over_z(j):
-        value = part3[j, z].astype(jnp.float32)
+        value = keep3[j]
         for s in range(1, zs):
             landed(recv3.at[j, s - 1], s3_in.at[j, s - 1])
             value += recv3[j, s - 1].astype(jnp.float32)
@@ -306,6 +360,26 @@
     totals[...] = jnp.broadcast_to(count, totals.shape)
     for copy in sent:
         copy.wait_send()
+
+    def z_sent(source, carry):
+        @pl.when(jnp.logical_and(above, source <= z))
+        def _():
+            passed(source)
+
+        @pl.when(jnp.logical_and(below, source >= z))
+        def _():
+            passed(zs + source)
+
+        passed(2 * zs + source)
+        return carry
+
+    lax.fori_loop(0, zs, z_sent, 0)
+
+    def mate_sent(i, carry):
+        passed(3 * zs + i)
+        return carry
+
+    lax.fori_loop(0, slots // 2, mate_sent, 0)
 
 
 def group_scratch(zs, rows, width, ff, experts):
@@ -320,11 +394,14 @@
         ((ff, width), bf),
         ((chunks, ff, cd), bf),
         ((slots, rows, 2 * ff), bf),
-        ((chunks, 2, slots // 2, rows, cd), bf),
         ((chunks, slots // 2, rows, cd), bf),
+        ((chunks, slots // 2, rows, cd), f32),
         ((chunks, slots // 2, rows, cd), bf),
         ((chunks, zs, rows, cd), bf),
+        ((chunks, zs, rows, cd), f32),
         ((chunks, zs, rows, cd), bf),
+        ((chunks, zs - 1, rows, cd), bf),
+        ((chunks, rows, cd), f32),
         ((chunks, zs - 1, rows, cd), bf),
         ((experts, rows), f32),
         ((experts, rows), f32),
@@ -355,8 +432,8 @@
             for shape, kind in group_scratch(zs, rows, width, ff, experts)
         ]
         + [
-            dma((slots,)), dma((slots,)), dma((slots,)), dma((slots,)), dma((4,)),
-            dma((2,)), dma((2,)), dma((chunks,)), dma((chunks,)),
+            dma((slots,)), dma((5 * zs,)), dma((slots,)), dma((5 * zs,)), dma((4,)),
+            dma((2, per_device)), dma((2, per_device)), dma((chunks,)), dma((chunks,)),
             dma((chunks,)), dma((chunks,)), dma((chunks,)), dma((chunks,)),
             dma((chunks, zs - 1)), dma((chunks, zs - 1)), dma, dma,
         ],

time: 162 us -> 148 us (0.914)
  Pallas kernels: 156 us -> 141 us
    pallas_call x1, Pallas kernels: 156 us -> 141 us  [group_body(): pl.pallas_call(functools.partial(layer_kernel, zs, capacity, per_device),...]
where the time goes in v2:
time: 148 us; the launch traced here: 147 us
  Pallas kernels  141 us (95%)
  other arithmetic  3.31 us (2%)
  local copies, waits for them, and re-layouts  1.88 us (1%)
    pallas_call x1, Pallas kernels, group_body(): pl.pallas_call(functools.partial(layer_kernel, zs, capacity, per_device),...  141 us

profile of v2, /device:TPU:0, one launch (start us, length us, event | category | flops | bytes accessed | tf_op | source)
XLA Modules:
  0.0 147.2 jit_solution(373770698933702295)
XLA Ops:
  0.6 141.4 %shard_map.94 = (bf16[128,2048]{1,0:T(8,128)(2,1)}, f32[16,128]{1,0:T(8,128)}) custom-call(bf16[128,2048]{1,0:T(8,128)(2,1)} %tokens.1, s32[8,128]{1,0:T(8,128)} %bitcast.8, f32[8,128]{1,0:T(8,128)} %bitcast.9, bf16[384,2048]{1,0:T(8,128)(2,1)} %bitcast.5, bf16[384,2048]{1,0:T(8,128)(2,1)} %bitcast.6, bf16[384,2048]{1,0:T(8,128)(2,1)} %bitcast.7), custom_call_target="tpu_custom_call" | custom-call | tf_op jit(solution)/shard_map/pallas_call | solution.py:422
  142.0 0.8 multiply_reduce_fusion
  142.9 1.2 add.3
  144.0 1.3 convert_reduce_fusion
  145.4 1.9 %copy.11 = bf16[128,2048]{1,0:T(8,128)(2,1)} copy(bf16[128,2048]{1,0:T(8,128)(2,1)} %get-tuple-element.10) | data formatting | bytes 1048576

commit v3 on v2

--- a/solution.py
+++ b/solution.py
@@ -274,7 +274,7 @@
         landed(gate_w.at[1, units], w_in.at[0, j])
         landed(up_w.at[1, units], w_in.at[1, j])
 
-        def other_half(q, carry):
+        def other_half(q, carry, j=j):
             first = q * batch
             block = tok[pl.ds(first, batch)].reshape(batch * rows, width)
             value = act(block, gate_w[1, j * unit : (j + 1) * unit], up_w[1, j * unit : (j + 1) * unit])
@@ -285,11 +285,13 @@
                 )
             return carry
 
-        lax.fori_loop(0, slots // batch, other_half, 0)
-
-    def down(j):
-        landed(down_far.at[j], d_in.at[j])
-
+        if j < per_device - 1:
+            lax.fori_loop(0, slots // batch, other_half, 0)
+
+    groups = slots // batch // 2
+    starts = ((1 - y) * groups, y * groups)
+
+    def down(j, part):
         def step(q, carry):
             near = hidden[pl.ds(q * batch, batch)].reshape(batch * rows, 2 * ff)
             value = jnp.dot(
@@ -303,11 +305,14 @@
                 part1[j, q * (batch // 2) + i] = jnp.where(c == 0, two, one).astype(jnp.bfloat16)
             return carry
 
-        lax.fori_loop(0, slots // batch, step, 0)
-        remote(part1.at[j], recv1.at[j], s1_out.at[j], s1_in.at[j], mate)
+        lax.fori_loop(starts[part], starts[part] + groups, step, 0)
+        held = pl.ds(starts[part] * (batch // 2), zs)
+        remote(
+            part1.at[j, held], recv1.at[j, held], s1_out.at[j, part], s1_in.at[j, part], mate
+        )
 
     def over_core(j):
-        landed(recv1.at[j], s1_in.at[j])
+        landed(recv1.at[j, pl.ds((1 - y) * zs, zs)], s1_in.at[j, 0])
 
         def away(i, carry):
             n = (1 - y) * zs + i
@@ -317,6 +322,8 @@
 
         lax.fori_loop(0, zs, away, 0)
         remote(part2.at[j], recv2.at[j], s2_out.at[j], s2_in.at[j], y_side)
+
+        landed(recv1.at[j, pl.ds(y * zs, zs)], s1_in.at[j, 1])
 
         def home(i, carry):
             n = y * zs + i
@@ -347,7 +354,14 @@
 
     for j in range(chunks + 3):
         if j < chunks:
-            down(j)
+            if j > 0:
+                landed(down_far.at[j], d_in.at[j])
+            for part in range(2):
+                if j == 0:
+                    lax.fori_loop(starts[part], starts[part] + groups, other_half, 0)
+                    if part == 0:
+                        landed(down_far.at[0], d_in.at[0])
+                down(j, part)
         if 0 <= j - 1 < chunks:
             over_core(j - 1)
         if 0 <= j - 2 < chunks:
@@ -434,7 +448,7 @@
         + [
             dma((slots,)), dma((5 * zs,)), dma((slots,)), dma((5 * zs,)), dma((4,)),
             dma((2, per_device)), dma((2, per_device)), dma((chunks,)), dma((chunks,)),
-            dma((chunks,)), dma((chunks,)), dma((chunks,)), dma((chunks,)),
+            dma((chunks, 2)), dma((chunks, 2)), dma((chunks,)), dma((chunks,)),
             dma((chunks, zs - 1)), dma((chunks, zs - 1)), dma, dma,
         ],
         compiler_params=pltpu.CompilerParams(
@@ -463,7 +477,7 @@
             size *= extent
         total += size
     args = (tokens, routes, route_weight, bias, w_gate, w_up, w_down)
-    if lax.axis_size("dp") == 4 and groups % 2 == 0 and zs > 1 and total < 0.85 * VMEM_BYTES:
+    if lax.axis_size("dp") == 4 and groups % 2 == 0 and zs % 2 == 0 and total < 0.85 * VMEM_BYTES:
         return group_body(zs, *args)
     return exchange_body(*args)
 

time: 148 us -> 146 us (0.986)
    pallas_call x1, Pallas kernels: 141 us -> 140 us  [group_body(): pl.pallas_call(functools.partial(layer_kernel, zs, capacity, per_device),...]
where the time goes in v3:
time: 146 us
  Pallas kernels  140 us (96%)
  other arithmetic  3.31 us (2%)
  local copies, waits for them, and re-layouts  1.88 us (1%)
    pallas_call x1, Pallas kernels, group_body(): pl.pallas_call(functools.partial(layer_kernel, zs, capacity, per_device),...  140 us

profile of v3, /device:TPU:0, one launch (start us, length us, event | category | flops | bytes accessed | tf_op | source)
XLA Modules:
  0.0 145.6 jit_solution(8196577129015364851)
XLA Ops:
  0.6 139.8 %shard_map.94 = (bf16[128,2048]{1,0:T(8,128)(2,1)}, f32[16,128]{1,0:T(8,128)}) custom-call(bf16[128,2048]{1,0:T(8,128)(2,1)} %tokens.1, s32[8,128]{1,0:T(8,128)} %bitcast.8, f32[8,128]{1,0:T(8,128)} %bitcast.9, bf16[384,2048]{1,0:T(8,128)(2,1)} %bitcast.5, bf16[384,2048]{1,0:T(8,128)(2,1)} %bitcast.6, bf16[384,2048]{1,0:T(8,128)(2,1)} %bitcast.7), custom_call_target="tpu_custom_call" | custom-call | tf_op jit(solution)/shard_map/pallas_call | solution.py:436
  140.4 0.8 multiply_reduce_fusion
  141.2 1.2 add.3
  142.4 1.3 convert_reduce_fusion
  143.7 1.9 %copy.11 = bf16[128,2048]{1,0:T(8,128)(2,1)} copy(bf16[128,2048]{1,0:T(8,128)(2,1)} %get-tuple-element.10) | data formatting | bytes 1048576
